TPU v7x, 32 devices: a whole 2x2x4 slice. The times are simulated.
32 devices in a mesh: strip: 8 (over z, x), col: 4 (over y, core).
Axes of the slice: x: 2, y: 2, z: 4, core: 2. Of those that a mesh axis runs over, the one named last changes fastest.
Arguments:
- residuals: float32 [16, 64, 2560], P('strip'), may hold values from -6 to 6
- corr_rows: float32 [64], replicated, may hold values from 0.5 to 2
- corr_cols: float32 [2560], replicated, may hold values from 0.5 to 2
- row_anchor: int32 [16], replicated, may hold values from 0 to 64
- col_anchor: int32 [16], replicated, may hold values from 0 to 7680
- valid_first: int32 [16], replicated, may hold values from 0 to 15
- valid_end: int32 [16], replicated, may hold values from 49 to 64
- facet_of_slot: int32 [16], replicated, may hold values from 0 to 15, each once
Outputs:
- stitched: float32 [128, 10240], P('strip', 'col')
- column_power: float32 [10240], P('col')
Inputs may be any that keep to these rules, and one draw needn't show every extreme that they name: facet_of_slot names each of the 16 facets exactly once.
All inputs are finite; a program needn't handle non-finite values.
Results may differ from a plain program's by a relative error of at most 0.0003.
Values sent between devices are 32-bit elements; how exact they have to be, the bound alone decides.
No kernel may reach another device: no remote copies, remote signals or barrier semaphores. Data moves between devices by JAX's collectives and lax.ppermute only.
A program may use at most 64 MiB of HBM per device.

v0:
```python
import jax
import jax.numpy as jnp
from jax import lax
from jax.sharding import PartitionSpec as P


def tapers(count):
    position = (jnp.arange(count).astype(jnp.float32) + 0.5) / count
    return jnp.sin(jnp.pi * position) ** 2


def body(
    residuals, corr_rows, corr_cols, row_anchor, col_anchor, valid_first, valid_end, facet_of_slot
):
    local_count, facet_rows, facet_cols = residuals.shape
    strip_count = lax.axis_size("strip")
    strip_rows = facet_rows // 4
    image_rows = strip_count * strip_rows
    strip_index = lax.axis_index("strip")
    group_index = lax.axis_index("col")
    row_index = jnp.arange(facet_rows)
    row_taper = tapers(facet_rows)
    col_taper = tapers(facet_cols)
    correction = corr_rows[:, None] * corr_cols[None, :]
    side_blank = jnp.zeros((facet_rows, facet_cols), jnp.float32)
    num_bands = []
    for position in range(local_count):
        facet_id = facet_of_slot[strip_index * local_count + position]
        inside = (row_index >= valid_first[facet_id]) & (row_index < valid_end[facet_id])
        row_weight = jnp.where(inside, row_taper, 0.0)
        weight = row_weight[:, None] * col_taper[None, :]
        col_start = jnp.clip(
            group_index * facet_cols - col_anchor[facet_id] + facet_cols, 0, 2 * facet_cols
        )
        padded = jnp.concatenate(
            [side_blank, weight * correction * residuals[position], side_blank], axis=1
        )
        shifted = lax.dynamic_slice_in_dim(padded, col_start, facet_cols, 1)
        canvas = jnp.zeros((image_rows, facet_cols), jnp.float32)
        canvas = lax.dynamic_update_slice(canvas, shifted, (row_anchor[facet_id], 0))
        num_bands.append(canvas.reshape(strip_count, strip_rows, facet_cols))
    num_send = jnp.stack(num_bands, axis=1)
    got_num = lax.all_to_all(num_send, "strip", split_axis=0, concat_axis=0, tiled=True)
    facet_ids = jnp.arange(facet_of_slot.shape[0])
    row_local = strip_index * strip_rows + jnp.arange(strip_rows)
    row_pos = row_local[None, :] - row_anchor[:, None]
    row_inside = (row_pos >= valid_first[:, None]) & (row_pos < valid_end[:, None])
    row_value = jnp.sin(jnp.pi * (row_pos.astype(jnp.float32) + 0.5) / facet_rows) ** 2
    row_part = jnp.where(row_inside, row_value, 0.0)
    col_local = group_index * facet_cols + jnp.arange(facet_cols)
    col_pos = col_local[None, :] - col_anchor[facet_ids][:, None]
    col_inside = (col_pos >= 0) & (col_pos < facet_cols)
    col_value = jnp.sin(jnp.pi * (col_pos.astype(jnp.float32) + 0.5) / facet_cols) ** 2
    col_part = jnp.where(col_inside, col_value, 0.0)
    denominator = jnp.einsum("fv,fu->vu", row_part, col_part, precision=lax.Precision.HIGHEST)
    numerator = jnp.sum(got_num, axis=(0, 1))
    stitched = numerator / jnp.maximum(denominator, 0.5)
    column_sums = lax.psum(jnp.sum(stitched * stitched, axis=0), "strip")
    return (stitched, column_sums / image_rows)


def solution(mesh):
    in_specs = (P("strip", None, None), P(), P(), P(), P(), P(), P(), P())
    out_specs = (P("strip", "col"), P("col"))
    return jax.shard_map(body, mesh=mesh, in_specs=in_specs, out_specs=out_specs, check_vma=False)
```

profile of v0, /device:TPU:0, one launch (start us, length us, event | category | flops | bytes accessed | tf_op | source)
XLA Modules:
  0.0 127.8 jit_solution(10135443065391539872)
XLA Ops:
  0.6 1.3 %fusion.47 = (s32[1]{0:T(128)}, s32[1]{0:T(128)}) fusion(s32[16]{0:T(128)} %param.15, s32[]{:T(128)S(6)} %select_n.50, s32[]{:T(128)S(6)} %select_n.54), kind=kLoop, calls=%fused_computation.69 | loop fusion | bytes 24 | tf_op jit(solution)/shard_map/dynamic_slice | solution.py:28
  4.6 0.1 sine_multiply_fusion
  5.9 1.4 %fusion.43 = (s32[1]{0:T(128)}, s32[1]{0:T(128)}, s32[1]{0:T(128)}, s32[1]{0:T(128)}) fusion(s32[16]{0:T(128)} %param.11, s32[]{:T(128)S(6)} %select_n.51, s32[]{:T(128)S(6)} %select_n.55, s32[16]{0:T(128)} %param.13), kind=kLoop, calls=%fused_computation.65 | loop fusion | bytes 40 | tf_op jit(solution)/shard_map/dynamic_slice | solution.py:40
  9.8 1.4 %fusion.45 = (s32[1]{0:T(128)}, s32[1]{0:T(128)}, s32[1]{0:T(128)}, s32[1]{0:T(128)}) fusion(s32[16]{0:T(128)} %param.14, s32[]{:T(128)S(6)} %select_n.51, s32[]{:T(128)S(6)} %select_n.55, s32[16]{0:T(128)} %param.12), kind=kLoop, calls=%fused_computation.67 | loop fusion | bytes 40 | tf_op jit(solution)/shard_map/dynamic_slice | solution.py:29
  12.5 1.2 and_select_fusion
  13.7 1.4 %and_select_fusion.1 = f32[64]{0:T(128)S(1)} fusion(s32[]{:T(128)} %bitcast.2, s32[]{:T(128)} %bitcast.1), kind=kLoop, calls=%fused_computation.56 | loop fusion | flops 512 | bytes 264 | tf_op jit(solution)/shard_map/jit(_where)/select_n | solution.py:30
  16.3 1.5 %fusion.1 = (f32[64,2560]{1,0:T(8,128)S(1)}, f32[64,2560]{1,0:T(8,128)S(1)}) fusion(f32[2,64,2560]{2,1,0:T(8,128)} %param.8, f32[2560]{0:T(1024)} %param.10, f32[64]{0:T(128)} %param.9, f32[2560]{0:T(1024)S(1)} %sine_multiply_fusion, f32[64]{0:T(128)S(1)} %and_select_fusion.1, f32[64]{0:T(128)S(1)} %and_select_fusion), kind=kLoop, calls=%fused_computation.12 | loop fusion | flops 1146880 | bytes 2642688 | tf_op jit(solution)/shard_map/mul | solution.py:36
  17.9 1.1 fusion.6
  19.0 0.1 broadcast.78.clone.1
  19.2 1.1 dynamic_update_slice.6
  20.3 0.1 broadcast.78.clone
  20.4 1.0 dynamic_update_slice.7
  21.4 1.7 %pad_maximum_fusion = f32[8,2,16,2560]{3,2,1,0:T(8,128)} fusion(f32[8,1,16,2560]{3,2,1,0:T(8,128)S(1)} %bitcast.16, f32[8,1,16,2560]{3,2,1,0:T(8,128)S(1)} %bitcast.17), kind=kLoop, calls=%fused_computation.7 | loop fusion | flops 655360 | bytes 5242880 | tf_op jit(solution)/shard_map/stack | solution.py:42
  23.2 0.0 copy-start
  23.2 7.5 %all-to-all-start = ((f32[8,2,16,2560]{3,2,1,0:T(8,128)}), f32[8,2,16,2560]{3,2,1,0:T(8,128)S(1)}, u32[]{:S(2)}, u32[]{:S(2)}) async-start(f32[8,2,16,2560]{3,2,1,0:T(8,128)} %pad_maximum_fusion), calls=%async_computation | async-start | bytes 5242880 | tf_op jit(solution)/shard_map/all_to_all | solution.py:43
  30.7 0.0 copy-start.1
  30.7 0.0 copy-start.2
  30.7 0.0 copy-start.3
  30.7 0.0 copy-done
  30.8 0.7 gather_fusion
  31.4 58.7 %all-to-all-done = f32[8,2,16,2560]{3,2,1,0:T(8,128)S(1)} async-done(((f32[8,2,16,2560]{3,2,1,0:T(8,128)}), f32[8,2,16,2560]{3,2,1,0:T(8,128)S(1)}, u32[]{:S(2)}, u32[]{:S(2)}) %all-to-all-start) | async-done | bytes 2621472 | tf_op jit(solution)/shard_map/all_to_all | solution.py:43
  90.2 0.1 reduce_sum.18
  90.3 0.0 copy-done.1
  90.3 0.0 copy-done.2
  90.3 0.0 copy-done.3
  90.3 1.6 %multiply_reduce_fusion = (f32[2560]{0:T(1024)S(1)}, f32[16,2560]{1,0:T(8,128)}) fusion(f32[16,2560]{1,0:T(8,128)S(1)} %reduce_sum.18, s32[16]{0:T(128)S(1)} %gather_fusion, s32[2560]{0:T(1024)S(1)} %iota_add_fusion, s32[16]{0:T(128)S(1)} %copy-done.1, s32[16]{0:T(128)S(1)} %copy-done.3, s32[16]{0:T(128)S(1)} %copy-done.2, s32[16]{0:T(128)S(1)} %iota_add_fusion.1), kind=kOutput, calls=%fused_computation.26 | convolution fusion | flops 8396544 | bytes 348480 | tf_op jit(solution)/shard_map/fv,fu->vu/dot_general | solution.py:55
  92.0 35.2 %psum.7 = f32[2560]{0:T(1024)S(1)} all-reduce(f32[2560]{0:T(1024)S(1)} %get-tuple-element.16), channel_id=1, replica_groups=mesh['strip'=8,'col'=4] {'strip'}, use_global_device_ids=true, to_apply=%region_2.3 | all-reduce | flops 2560 | bytes 20480 | tf_op jit(solution)/shard_map/psum | solution.py:58
  127.2 0.6 broadcast_multiply_fusion
  (5 shorter events, 0.1 us)
Async XLA Ops:
  23.2 7.6 %copy-start = (s32[16]{0:T(128)S(1)}, s32[16]{0:T(128)}, u32[]{:S(2)}) copy-start(s32[16]{0:T(128)} %param.12) | copy-start | bytes 196
  23.2 67.0 %all-to-all-start = ((f32[8,2,16,2560]{3,2,1,0:T(8,128)}), f32[8,2,16,2560]{3,2,1,0:T(8,128)S(1)}, u32[]{:S(2)}, u32[]{:S(2)}) async-start(f32[8,2,16,2560]{3,2,1,0:T(8,128)} %pad_maximum_fusion), calls=%async_computation | async-start | bytes 5242880 | tf_op jit(solution)/shard_map/all_to_all | solution.py:43
  30.7 59.6 %copy-start.1 = (s32[16]{0:T(128)S(1)}, s32[16]{0:T(128)}, u32[]{:S(2)}) copy-start(s32[16]{0:T(128)} %param.14) | copy-start | bytes 196
  30.7 59.6 %copy-start.2 = (s32[16]{0:T(128)S(1)}, s32[16]{0:T(128)}, u32[]{:S(2)}) copy-start(s32[16]{0:T(128)} %param.11) | copy-start | bytes 196
  30.7 59.6 %copy-start.3 = (s32[16]{0:T(128)S(1)}, s32[16]{0:T(128)}, u32[]{:S(2)}) copy-start(s32[16]{0:T(128)} %param.13) | copy-start | bytes 196
where the time goes:
time: 128 us
  waiting for transfers between devices  58.7 us (46%)
  blocking collectives  35.2 us (28%)
  between operations  9.63 us (8%)
  other arithmetic  7.82 us (6%)
  starting transfers between devices  7.53 us (6%)
  local copies, waits for them, and re-layouts  7.23 us (6%)
  matrix products  1.64 us (1%)
    all_to_all x1, waiting for transfers between devices, body(): lax.all_to_all(num_send, 'strip', split_axis=0, concat_axis=0, tiled=True)  58.7 us
    psum x1, blocking collectives, body(): column_sums = lax.psum(jnp.sum(stitched * stitched, axis=0), 'strip')  35.2 us
    all_to_all x1, starting transfers between devices, body(): lax.all_to_all(num_send, 'strip', split_axis=0, concat_axis=0, tiled=True)  7.53 us
    select_n x2, other arithmetic, body(): row_weight = jnp.where(inside, row_taper, 0.0)  2.63 us
  transfers between devices with their start and end apart: 1, of which 1 were waited for; matrix products, arithmetic and copies ran while one was open for 1% of the time, Pallas kernels for 0%

commit v1 on v0

--- a/solution.py
+++ b/solution.py
@@ -1,7 +1,17 @@
+import functools
 import jax
 import jax.numpy as jnp
 from jax import lax
 from jax.sharding import PartitionSpec as P
+from jax.lax import all_gather
+
+
+def _list_outputs(page, ax_name):
+    arr_now = all_gather(page, axis_name=ax_name).sum(axis=0)
+    return arr_now
+
+
+touch_ratios_here = functools.partial(_list_outputs, ax_name="strip")
 
 
 def tapers(count):
@@ -55,7 +65,7 @@
     denominator = jnp.einsum("fv,fu->vu", row_part, col_part, precision=lax.Precision.HIGHEST)
     numerator = jnp.sum(got_num, axis=(0, 1))
     stitched = numerator / jnp.maximum(denominator, 0.5)
-    column_sums = lax.psum(jnp.sum(stitched * stitched, axis=0), "strip")
+    column_sums = touch_ratios_here(jnp.sum(stitched * stitched, axis=0))
     return (stitched, column_sums / image_rows)
 
 

time: 128 us -> 124 us (0.969)
  blocking collectives: 35.2 us -> 30.5 us
    psum x1 -> x0, blocking collectives: 35.2 us -> none  [body(): column_sums = lax.psum(jnp.sum(stitched * stitched, axis=0), 'strip')]
    all_gather x0 -> x1, blocking collectives: none -> 30.5 us  [_list_outputs(): arr_now = all_gather(page, axis_name=ax_name).sum(axis=0)]
where the time goes in v1:
time: 124 us; the launch traced here: 123 us
  waiting for transfers between devices  58.7 us (47%)
  blocking collectives  30.5 us (25%)
  between operations  9.63 us (8%)
  other arithmetic  7.89 us (6%)
  starting transfers between devices  7.53 us (6%)
  local copies, waits for them, and re-layouts  7.23 us (6%)
  matrix products  1.64 us (1%)
    all_to_all x1, waiting for transfers between devices, body(): lax.all_to_all(num_send, 'strip', split_axis=0, concat_axis=0, tiled=True)  58.7 us
    all_gather x1, blocking collectives, _list_outputs(): arr_now = all_gather(page, axis_name=ax_name).sum(axis=0)  30.5 us
    all_to_all x1, starting transfers between devices, body(): lax.all_to_all(num_send, 'strip', split_axis=0, concat_axis=0, tiled=True)  7.53 us
    select_n x2, other arithmetic, body(): row_weight = jnp.where(inside, row_taper, 0.0)  2.63 us
  transfers between devices with their start and end apart: 1, of which 1 were waited for; matrix products, arithmetic and copies ran while one was open for 1% of the time, Pallas kernels for 0%

profile of v1, /device:TPU:0, one launch (start us, length us, event | category | flops | bytes accessed | tf_op | source)
XLA Modules:
  0.0 123.2 jit_solution(15755452113020551008)
XLA Ops:
  0.6 1.3 %fusion.47 = (s32[1]{0:T(128)}, s32[1]{0:T(128)}) fusion(s32[16]{0:T(128)} %param.15, s32[]{:T(128)S(6)} %select_n.50, s32[]{:T(128)S(6)} %select_n.54), kind=kLoop, calls=%fused_computation.69 | loop fusion | bytes 24 | tf_op jit(solution)/shard_map/dynamic_slice | solution.py:38
  4.6 0.1 sine_multiply_fusion
  5.9 1.4 %fusion.43 = (s32[1]{0:T(128)}, s32[1]{0:T(128)}, s32[1]{0:T(128)}, s32[1]{0:T(128)}) fusion(s32[16]{0:T(128)} %param.11, s32[]{:T(128)S(6)} %select_n.51, s32[]{:T(128)S(6)} %select_n.55, s32[16]{0:T(128)} %param.13), kind=kLoop, calls=%fused_computation.65 | loop fusion | bytes 40 | tf_op jit(solution)/shard_map/dynamic_slice | solution.py:50
  9.8 1.4 %fusion.45 = (s32[1]{0:T(128)}, s32[1]{0:T(128)}, s32[1]{0:T(128)}, s32[1]{0:T(128)}) fusion(s32[16]{0:T(128)} %param.14, s32[]{:T(128)S(6)} %select_n.51, s32[]{:T(128)S(6)} %select_n.55, s32[16]{0:T(128)} %param.12), kind=kLoop, calls=%fused_computation.67 | loop fusion | bytes 40 | tf_op jit(solution)/shard_map/dynamic_slice | solution.py:39
  12.5 1.2 %and_select_fusion = f32[64]{0:T(128)S(1)} fusion(s32[]{:T(128)} %bitcast.9, s32[]{:T(128)} %bitcast.8), kind=kLoop, calls=%fused_computation.55 | loop fusion | flops 512 | bytes 264 | tf_op jit(solution)/shard_map/jit(_where)/select_n | solution.py:40
  13.7 1.4 %and_select_fusion.1 = f32[64]{0:T(128)S(1)} fusion(s32[]{:T(128)} %bitcast.2, s32[]{:T(128)} %bitcast.1), kind=kLoop, calls=%fused_computation.56 | loop fusion | flops 512 | bytes 264 | tf_op jit(solution)/shard_map/jit(_where)/select_n | solution.py:40
  16.3 1.5 %fusion.1 = (f32[64,2560]{1,0:T(8,128)S(1)}, f32[64,2560]{1,0:T(8,128)S(1)}) fusion(f32[2,64,2560]{2,1,0:T(8,128)} %param.8, f32[2560]{0:T(1024)} %param.10, f32[64]{0:T(128)} %param.9, f32[2560]{0:T(1024)S(1)} %sine_multiply_fusion, f32[64]{0:T(128)S(1)} %and_select_fusion.1, f32[64]{0:T(128)S(1)} %and_select_fusion), kind=kLoop, calls=%fused_computation.12 | loop fusion | flops 1146880 | bytes 2642688 | tf_op jit(solution)/shard_map/mul | solution.py:46
  17.9 1.1 fusion.6
  19.0 0.1 broadcast.78.clone.1
  19.2 1.1 dynamic_update_slice.6
  20.3 0.1 broadcast.78.clone
  20.4 1.0 dynamic_update_slice.7
  21.4 1.7 %pad_maximum_fusion = f32[8,2,16,2560]{3,2,1,0:T(8,128)} fusion(f32[8,1,16,2560]{3,2,1,0:T(8,128)S(1)} %bitcast.16, f32[8,1,16,2560]{3,2,1,0:T(8,128)S(1)} %bitcast.17), kind=kLoop, calls=%fused_computation.7 | loop fusion | flops 655360 | bytes 5242880 | tf_op jit(solution)/shard_map/stack | solution.py:52
  23.2 0.0 copy-start
  23.2 7.5 %all-to-all-start = ((f32[8,2,16,2560]{3,2,1,0:T(8,128)}), f32[8,2,16,2560]{3,2,1,0:T(8,128)S(1)}, u32[]{:S(2)}, u32[]{:S(2)}) async-start(f32[8,2,16,2560]{3,2,1,0:T(8,128)} %pad_maximum_fusion), calls=%async_computation | async-start | bytes 5242880 | tf_op jit(solution)/shard_map/all_to_all | solution.py:53
  30.7 0.0 copy-start.1
  30.7 0.0 copy-start.2
  30.7 0.0 copy-start.3
  30.7 0.0 copy-done
  30.8 0.7 gather_fusion
  31.4 58.7 %all-to-all-done = f32[8,2,16,2560]{3,2,1,0:T(8,128)S(1)} async-done(((f32[8,2,16,2560]{3,2,1,0:T(8,128)}), f32[8,2,16,2560]{3,2,1,0:T(8,128)S(1)}, u32[]{:S(2)}, u32[]{:S(2)}) %all-to-all-start) | async-done | bytes 2621472 | tf_op jit(solution)/shard_map/all_to_all | solution.py:53
  90.2 0.1 reduce_sum.27
  90.3 0.0 copy-done.1
  90.3 0.0 copy-done.2
  90.3 0.0 copy-done.3
  90.3 1.6 %multiply_reduce_fusion = (f32[2560]{0:T(1024)S(1)}, f32[16,2560]{1,0:T(8,128)}) fusion(f32[16,2560]{1,0:T(8,128)S(1)} %reduce_sum.27, s32[16]{0:T(128)S(1)} %gather_fusion, s32[2560]{0:T(1024)S(1)} %iota_add_fusion, s32[16]{0:T(128)S(1)} %copy-done.1, s32[16]{0:T(128)S(1)} %copy-done.3, s32[16]{0:T(128)S(1)} %copy-done.2, s32[16]{0:T(128)S(1)} %iota_add_fusion.1), kind=kOutput, calls=%fused_computation.26 | convolution fusion | flops 8396544 | bytes 348480 | tf_op jit(solution)/shard_map/fv,fu->vu/dot_general | solution.py:65
  92.0 30.5 %all-gather.1 = f32[8,1,2560]{2,1,0:T(1,128)S(1)} all-gather(f32[1,1,2560]{2,1,0:T(1,128)S(1)} %reshape.61), channel_id=2, replica_groups=mesh['strip'=8,'col'=4] {'strip'}, dimensions={0}, use_global_device_ids=true | all-gather | bytes 92160 | tf_op jit(solution)/shard_map/all_gather | solution.py:10
  122.5 0.1 reduce_sum.29
  122.6 0.6 broadcast_multiply_fusion
  (6 shorter events, 0.1 us)
Async XLA Ops:
  23.2 7.6 %copy-start = (s32[16]{0:T(128)S(1)}, s32[16]{0:T(128)}, u32[]{:S(2)}) copy-start(s32[16]{0:T(128)} %param.12) | copy-start | bytes 196
  23.2 67.0 %all-to-all-start = ((f32[8,2,16,2560]{3,2,1,0:T(8,128)}), f32[8,2,16,2560]{3,2,1,0:T(8,128)S(1)}, u32[]{:S(2)}, u32[]{:S(2)}) async-start(f32[8,2,16,2560]{3,2,1,0:T(8,128)} %pad_maximum_fusion), calls=%async_computation | async-start | bytes 5242880 | tf_op jit(solution)/shard_map/all_to_all | solution.py:53
  30.7 59.6 %copy-start.1 = (s32[16]{0:T(128)S(1)}, s32[16]{0:T(128)}, u32[]{:S(2)}) copy-start(s32[16]{0:T(128)} %param.14) | copy-start | bytes 196
  30.7 59.6 %copy-start.2 = (s32[16]{0:T(128)S(1)}, s32[16]{0:T(128)}, u32[]{:S(2)}) copy-start(s32[16]{0:T(128)} %param.11) | copy-start | bytes 196
  30.7 59.6 %copy-start.3 = (s32[16]{0:T(128)S(1)}, s32[16]{0:T(128)}, u32[]{:S(2)}) copy-start(s32[16]{0:T(128)} %param.13) | copy-start | bytes 196
